TPU v7x, 32 devices: a whole 2x2x4 slice. The times are simulated.
32 devices in a mesh: cp: 32 (over z, y, x, core).
Axes of the slice: x: 2, y: 2, z: 4, core: 2. Of those that a mesh axis runs over, the one named last changes fastest.
Arguments:
- queries: bfloat16 [16384, 512], P('cp'), may hold values from -6 to 6
- keys: bfloat16 [16384, 128], P('cp'), may hold values from -6 to 6
- values: bfloat16 [16384, 128], P('cp'), may hold values from -6 to 6
- grad_out: bfloat16 [16384, 512], P('cp'), may hold values from -6 to 6
- selections: int32 [32, 2], P('cp'), may hold values from -1 to 30, as said below
Outputs:
- attended: bfloat16 [16384, 512], P('cp')
- grad_queries: bfloat16 [16384, 512], P('cp')
- grad_keys: bfloat16 [16384, 128], P('cp')
- grad_values: bfloat16 [16384, 128], P('cp')
Inputs may be any that keep to these rules, and one draw needn't show every extreme that they name: `selections`: row b names two different blocks before block b; where block b has fewer than two earlier blocks, the missing entries are -1 (blocks 0 and 1 only).
All inputs are finite; a program needn't handle non-finite values.
Results may differ from a plain program's by a relative error of at most 0.015.
Values may be sent and summed in bfloat16 or wider, within the bound.
No kernel may reach another device: no remote copies, remote signals or barrier semaphores. Data moves between devices by JAX's collectives and lax.ppermute only.
A program may use at most 128 MiB of HBM per device.

v0:
```python
import jax
import jax.numpy as jnp
from jax import lax
from jax.sharding import PartitionSpec as P

HEADS = 4
HEAD_DIM = 128
BLK = 512
masked_value = -1e30


def key_mask(chosen):
    rows_at = lax.broadcasted_iota(jnp.int32, (BLK, BLK), 0)
    cols_at = lax.broadcasted_iota(jnp.int32, (BLK, BLK), 1)
    causal = cols_at <= rows_at
    first_ok = jnp.broadcast_to(chosen[0] >= 0, (BLK, BLK))
    second_ok = jnp.broadcast_to(chosen[1] >= 0, (BLK, BLK))
    return jnp.concatenate([causal, first_ok, second_ok], axis=1)


def attend_forward(query_rows, block_keys, allowed):
    score_scale = HEAD_DIM ** (-0.5)
    query_heads = query_rows.reshape(BLK, HEADS, HEAD_DIM)
    scores = (
        jnp.einsum("qhd,kd->hqk", query_heads, block_keys, preferred_element_type=jnp.float32)
        * score_scale
    )
    scores = jnp.where(allowed[None], scores, masked_value)
    row_max = jnp.max(scores, axis=-1, keepdims=True)
    exponent = jnp.exp(scores - row_max)
    weights = exponent / jnp.sum(exponent, axis=-1, keepdims=True)
    return (query_heads, weights, weights.astype(jnp.bfloat16))


def body(queries, keys, values, grad_out, selections):
    devices = lax.axis_size("cp")
    local_rows = queries.shape[0]
    local_blocks = local_rows // BLK
    piece_rows = BLK // devices
    head_width = keys.shape[1]
    pair_width = 2 * head_width
    score_scale = HEAD_DIM ** (-0.5)
    requests = lax.all_gather(selections, "cp", axis=0, tiled=True)
    local_pairs = jnp.concatenate([keys, values], axis=1)

    def block_inputs(member, gathered):
        joined = jnp.concatenate(
            [local_pairs, gathered[2 * member], gathered[2 * member + 1]], axis=0
        )
        return (joined[:, :head_width], joined[:, head_width:], key_mask(selections[member]))

    spread = lax.all_to_all(
        local_pairs.reshape(local_blocks, devices, piece_rows, pair_width),
        "cp",
        split_axis=1,
        concat_axis=0,
        tiled=True,
    )
    held_pieces = spread.reshape(local_blocks * devices, piece_rows, pair_width)
    wanted = jnp.maximum(requests, 0)
    outgoing = held_pieces[wanted]
    arrived = lax.all_to_all(outgoing, "cp", split_axis=0, concat_axis=2, tiled=True)
    fetched = arrived.reshape(2 * local_blocks, BLK, pair_width)
    member = 0
    block_keys, block_values, allowed = block_inputs(member, fetched)
    query_heads, weights, probs_low = attend_forward(queries, block_keys, allowed)
    output_heads = jnp.einsum(
        "hqk,kd->qhd", probs_low, block_values, preferred_element_type=jnp.float32
    )
    attended = output_heads.astype(jnp.bfloat16).reshape(BLK, HEADS * HEAD_DIM)
    slot_grads = []
    member = 0
    block_keys, block_values, allowed = block_inputs(member, fetched)
    query_heads, weights, probs_low = attend_forward(queries, block_keys, allowed)
    grad_heads = grad_out.reshape(BLK, HEADS, HEAD_DIM)
    grad_probs = jnp.einsum(
        "qhd,kd->hqk", grad_heads, block_values, preferred_element_type=jnp.float32
    )
    inner_sum = jnp.sum(weights * grad_probs, axis=-1, keepdims=True)
    grad_scores = (weights * (grad_probs - inner_sum)).astype(jnp.bfloat16)
    grad_query = (
        jnp.einsum("hqk,kd->qhd", grad_scores, block_keys, preferred_element_type=jnp.float32)
        * score_scale
    )
    grad_queries = grad_query.astype(jnp.bfloat16).reshape(BLK, HEADS * HEAD_DIM)
    grad_k = (
        jnp.einsum("hqk,qhd->kd", grad_scores, query_heads, preferred_element_type=jnp.float32)
        * score_scale
    )
    grad_v = jnp.einsum("hqk,qhd->kd", probs_low, grad_heads, preferred_element_type=jnp.float32)
    grad_both = jnp.concatenate([grad_k, grad_v], axis=1)
    own_grads = grad_both[:BLK]
    slot_grads.append(grad_both[BLK : 2 * BLK])
    slot_grads.append(grad_both[2 * BLK :])
    partials = jnp.stack(slot_grads).reshape(2 * local_blocks, devices, piece_rows, pair_width)
    received = lax.all_to_all(
        partials.astype(jnp.bfloat16), "cp", split_axis=1, concat_axis=1, tiled=True
    ).astype(partials.dtype)
    owners_ids = requests.T.reshape(-1)
    total_blocks = devices * local_blocks
    onehot = (owners_ids[None, :] == jnp.arange(total_blocks, dtype=jnp.int32)[:, None]).astype(
        jnp.float32
    )
    summed = jnp.dot(
        onehot,
        received.reshape(2 * local_blocks * devices, piece_rows * pair_width),
        precision=lax.Precision.HIGHEST,
    )
    returned = lax.all_to_all(
        summed.reshape(devices, local_blocks, piece_rows, pair_width).astype(jnp.bfloat16),
        "cp",
        split_axis=0,
        concat_axis=2,
        tiled=True,
    ).astype(jnp.float32)
    grad_pairs = returned.reshape(local_rows, pair_width) + own_grads
    return (
        attended,
        grad_queries,
        grad_pairs[:, :head_width].astype(jnp.bfloat16),
        grad_pairs[:, head_width:].astype(jnp.bfloat16),
    )


def solution(mesh):
    in_specs = (P("cp", None), P("cp", None), P("cp", None), P("cp", None), P("cp", None))
    out_specs = (P("cp", None), P("cp", None), P("cp", None), P("cp", None))
    return jax.shard_map(body, mesh=mesh, in_specs=in_specs, out_specs=out_specs, check_vma=False)
```

profile of v0, /device:TPU:0, one launch (start us, length us, event | category | flops | bytes accessed | tf_op | source)
XLA Modules:
  0.0 151.7 jit_solution(15815537463073276769)
XLA Ops:
  0.6 1.6 %constant_dynamic-update-slice_fusion.1 = bf16[512,256]{1,0:T(8,128)(2,1)} fusion(bf16[512,128]{1,0:T(8,128)(2,1)} %param.6), kind=kLoop, calls=%fused_computation.49 | loop fusion | bytes 262144
  2.2 1.6 %constant_dynamic-update-slice_fusion = bf16[512,256]{1,0:T(8,128)(2,1)} fusion(bf16[512,256]{1,0:T(8,128)(2,1)} %constant_dynamic-update-slice_fusion.1, bf16[512,128]{1,0:T(8,128)(2,1)} %param.7), kind=kLoop, calls=%fused_computation.48 | loop fusion | bytes 262144 | tf_op jit(solution)/shard_map/concatenate | solution.py:44
  3.8 7.3 %all-to-all-start = ((bf16[1,32,16,256]{3,2,0,1:T(8,128)(2,1)}), bf16[1,32,16,256]{3,2,0,1:T(8,128)(2,1)S(1)}, u32[]{:S(2)}, u32[]{:S(2)}) async-start(bf16[1,32,16,256]{3,2,0,1:T(8,128)(2,1)} %bitcast.1), calls=%async_computation | async-start | bytes 524288 | tf_op jit(solution)/shard_map/all_to_all | solution.py:52
  11.1 42.0 %all-gather = s32[32,1,2]{2,1,0:T(1,128)S(1)} all-gather(s32[1,1,2]{2,1,0:T(1,128)} %bitcast.108), channel_id=1, replica_groups=mesh['cp'=32] {'cp'}, dimensions={0}, use_global_device_ids=true | all-gather | bytes 264 | tf_op jit(solution)/shard_map/all_gather | solution.py:43
  53.1 0.1 copy.48
  53.2 0.1 copy.49
  53.2 0.1 reshape.84
  53.4 0.0 all-to-all-done
  53.4 1.4 gather_fusion
  54.8 2.6 %all-to-all-start.1 = ((bf16[32,2,16,256]{3,2,1,0:T(8,128)(2,1)}), bf16[32,2,16,256]{3,2,1,0:T(8,128)(2,1)S(1)}, u32[]{:S(2)}, u32[]{:S(2)}) async-start(bf16[32,2,16,256]{3,2,1,0:T(8,128)(2,1)} %bitcast.5), calls=%async_computation.1 | async-start | bytes 1048576 | tf_op jit(solution)/shard_map/all_to_all | solution.py:62
  57.4 1.3 copy.80
  58.6 1.3 fusion.37
  61.3 1.3 copy.81
  62.6 0.1 iota_compare_fusion
  62.7 2.2 %add_add_fusion = pred[512,1536]{0,1:T(8,128)(4,1)} fusion(pred[512,512]{0,1:T(8,128)(4,1)S(1)} %iota_compare_fusion, pred[1536]{0:T(1024)(128)(4,1)S(1)} %pad.6.clone, pred[1536]{0:T(1024)(128)(4,1)S(1)} %pad.5.clone), kind=kLoop, calls=%fused_computation.18 | loop fusion | flops 1572864 | bytes 1051648 | tf_op jit(solution)/shard_map/concatenate | solution.py:18
  64.9 8.1 %all-to-all-done.1 = bf16[32,2,16,256]{3,2,1,0:T(8,128)(2,1)S(1)} async-done(((bf16[32,2,16,256]{3,2,1,0:T(8,128)(2,1)}), bf16[32,2,16,256]{3,2,1,0:T(8,128)(2,1)S(1)}, u32[]{:S(2)}, u32[]{:S(2)}) %all-to-all-start.1) | async-done | bytes 524320 | tf_op jit(solution)/shard_map/all_to_all | solution.py:62
  73.0 1.0 pad_maximum_fusion.1
  74.0 6.3 %fusion.28 = f32[1536,512,4]{1,0,2:T(8,128)} fusion(bf16[512,4,128]{0,2,1:T(8,128)(2,1)S(1)} %bitcast.96, bf16[1536,256]{1,0:T(8,128)(2,1)S(1)} %pad_maximum_fusion.1), kind=kOutput, calls=%fused_computation.42 | convolution fusion | flops 805306368 | bytes 13500416 | tf_op jit(solution)/shard_map/qhd,kd->hqk/dot_general | solution.py:25
  80.3 11.7 %fusion.38 = (f32[4,512]{1,0:T(4,128)S(1)}, f32[4,512,1536]{1,2,0:T(8,128)S(1)}) fusion(f32[1536,512,4]{1,0,2:T(8,128)} %fusion.28, pred[512,1536]{0,1:T(8,128)(4,1)} %add_add_fusion), kind=kOutput, calls=%fused_computation.57 | output fusion | flops 18875904 | bytes 25960448 | tf_op jit(solution)/shard_map/sub | solution.py:30
  92.0 0.0 copy-start.1
  92.0 5.9 %fusion.1 = (f32[4,512]{1,0:T(4,128)S(1)}, f32[1536,512,4]{1,0,2:T(8,128)}) fusion(f32[4,512,1536]{1,2,0:T(8,128)S(1)} %get-tuple-element.25, f32[4,512]{1,0:T(4,128)S(1)} %get-tuple-element.24, bf16[512,4,128]{0,2,1:T(8,128)(2,1)S(1)} %bitcast.105, bf16[1536,256]{1,0:T(8,128)(2,1)S(1)} %pad_maximum_fusion.1), kind=kOutput, calls=%fused_computation.4 | convolution fusion | flops 814741504 | bytes 26099712 | tf_op jit(solution)/shard_map/qhd,kd->hqk/dot_general | solution.py:76
  98.0 2.2 %fusion.12 = f32[1536,128]{0,1:T(8,128)S(1)} fusion(bf16[512,4,128]{0,2,1:T(8,128)(2,1)S(1)} %bitcast.106, f32[4,512,1536]{1,2,0:T(8,128)S(1)} %get-tuple-element.25, f32[4,512]{1,0:T(4,128)S(1)} %get-tuple-element.24), kind=kOutput, calls=%fused_computation.19 | convolution fusion | flops 811597824 | bytes 13901824 | tf_op jit(solution)/shard_map/hqk,qhd->kd/dot_general | solution.py:90
  100.2 0.0 copy-start.2
  100.2 0.1 copy-done.1
  100.3 6.8 %fusion.3 = bf16[4,512,1536]{1,2,0:T(8,128)(2,1)S(1)} fusion(f32[1536,512,4]{1,0,2:T(8,128)} %get-tuple-element.27, f32[4,512]{1,0:T(4,128)S(1)} %get-tuple-element.26, f32[4,512,1536]{1,2,0:T(8,128)S(1)} %get-tuple-element.25, f32[4,512]{1,0:T(4,128)S(1)} %get-tuple-element.24), kind=kLoop, calls=%fused_computation.6 | loop fusion | flops 12582912 | bytes 31473664 | tf_op jit(solution)/shard_map/convert_element_type | solution.py:80
  107.2 0.0 copy-start
  107.2 2.6 %copy-done = bf16[4,512,1536]{1,2,0:T(8,128)(2,1)} copy-done((bf16[4,512,1536]{1,2,0:T(8,128)(2,1)}, bf16[4,512,1536]{1,2,0:T(8,128)(2,1)S(1)}, u32[]{:S(2)}) %copy-start) | copy-done | bytes 6291480
  109.7 2.1 %fusion.15 = f32[1536,128]{0,1:T(8,128)S(1)} fusion(bf16[4,512,1536]{1,2,0:T(8,128)(2,1)S(1)} %fusion.3, bf16[512,4,128]{0,2,1:T(8,128)(2,1)S(1)} %bitcast.97), kind=kOutput, calls=%fused_computation.21 | convolution fusion | flops 805502976 | bytes 7602176 | tf_op jit(solution)/shard_map/hqk,qhd->kd/dot_general | solution.py:87
  111.9 0.0 copy-done.2
  111.9 0.0 copy-start.3
  111.9 0.1 fusion.16
  112.0 0.8 copy-done.3
  112.8 0.1 copy.60
  113.0 0.1 copy.61
  113.1 0.1 pad_maximum_fusion.2
  113.2 0.9 copy.62
  114.0 2.9 %all-to-all-start.2 = ((bf16[2,32,16,256]{3,2,0,1:T(8,128)(2,1)}), bf16[2,32,16,256]{3,2,0,1:T(8,128)(2,1)S(1)}, u32[]{:S(2)}, u32[]{:S(2)}) async-start(bf16[2,32,16,256]{3,2,0,1:T(8,128)(2,1)} %copy.62), calls=%async_computation.2 | async-start | bytes 1048576 | tf_op jit(solution)/shard_map/all_to_all | solution.py:96
  116.9 0.1 eq.15
  117.0 15.5 %all-to-all-done.2 = bf16[2,32,16,256]{3,2,0,1:T(8,128)(2,1)S(1)} async-done(((bf16[2,32,16,256]{3,2,0,1:T(8,128)(2,1)}), bf16[2,32,16,256]{3,2,0,1:T(8,128)(2,1)S(1)}, u32[]{:S(2)}, u32[]{:S(2)}) %all-to-all-start.2) | async-done | bytes 524320 | tf_op jit(solution)/shard_map/all_to_all | solution.py:96
  132.6 0.3 fusion.21
  132.8 0.0 slice-start
  132.8 0.9 copy.65
  133.7 3.5 %all-to-all-start.3 = ((bf16[32,1,16,256]{3,2,1,0:T(8,128)(2,1)}), bf16[32,1,16,256]{3,2,1,0:T(8,128)(2,1)}, u32[]{:S(2)}, u32[]{:S(2)}) async-start(bf16[32,1,16,256]{3,2,1,0:T(8,128)(2,1)} %copy.65), calls=%async_computation.3 | async-start | bytes 524288 | tf_op jit(solution)/shard_map/all_to_all | solution.py:109
  137.2 0.0 slice-start.1
  137.2 6.5 %fusion.18 = bf16[128,4,512]{2,0,1:T(8,128)(2,1)} fusion(bf16[1536,256]{1,0:T(8,128)(2,1)S(1)} %pad_maximum_fusion.1, f32[4,512,1536]{1,2,0:T(8,128)} %copy-done.1, f32[4,512]{1,0:T(4,128)S(1)} %get-tuple-element.24), kind=kOutput, calls=%fused_computation.28 | convolution fusion | flops 811859968 | bytes 13508608 | tf_op jit(solution)/shard_map/hqk,kd->qhd/dot_general | solution.py:67
  143.7 0.0 slice-done
  143.7 0.0 slice-done.1
  143.7 1.0 fusion.17
  144.8 1.0 copy.69
  145.8 2.0 %copy.68 = bf16[512,512]{1,0:T(8,128)(2,1)} copy(bf16[512,512]{0,1:T(8,128)(2,1)} %bitcast.107) | data formatting | bytes 1048576
  147.8 0.0 all-to-all-done.3
  147.8 1.0 bitcast_convert_fusion
  148.8 0.2 copy.67
  149.0 1.1 fusion.24
  150.1 0.8 copy.70
  150.9 0.8 copy.71
  (11 shorter events, 0.2 us)
Async XLA Ops:
  3.8 49.6 %all-to-all-start = ((bf16[1,32,16,256]{3,2,0,1:T(8,128)(2,1)}), bf16[1,32,16,256]{3,2,0,1:T(8,128)(2,1)S(1)}, u32[]{:S(2)}, u32[]{:S(2)}) async-start(bf16[1,32,16,256]{3,2,0,1:T(8,128)(2,1)} %bitcast.1), calls=%async_computation | async-start | bytes 524288 | tf_op jit(solution)/shard_map/all_to_all | solution.py:52
  54.8 18.2 %all-to-all-start.1 = ((bf16[32,2,16,256]{3,2,1,0:T(8,128)(2,1)}), bf16[32,2,16,256]{3,2,1,0:T(8,128)(2,1)S(1)}, u32[]{:S(2)}, u32[]{:S(2)}) async-start(bf16[32,2,16,256]{3,2,1,0:T(8,128)(2,1)} %bitcast.5), calls=%async_computation.1 | async-start | bytes 1048576 | tf_op jit(solution)/shard_map/all_to_all | solution.py:62
  92.0 8.3 %copy-start.1 = (f32[4,512,1536]{1,2,0:T(8,128)}, f32[4,512,1536]{1,2,0:T(8,128)S(1)}, u32[]{:S(2)}) copy-start(f32[4,512,1536]{1,2,0:T(8,128)S(1)} %get-tuple-element.25) | copy-start | bytes 37748740
  100.2 11.7 %copy-start.2 = (f32[1536,128]{0,1:T(8,128)}, f32[1536,128]{0,1:T(8,128)S(1)}, u32[]{:S(2)}) copy-start(f32[1536,128]{0,1:T(8,128)S(1)} %fusion.12) | copy-start | bytes 2359300
  107.2 2.6 %copy-start = (bf16[4,512,1536]{1,2,0:T(8,128)(2,1)}, bf16[4,512,1536]{1,2,0:T(8,128)(2,1)S(1)}, u32[]{:S(2)}) copy-start(bf16[4,512,1536]{1,2,0:T(8,128)(2,1)S(1)} %fusion.3) | copy-start | bytes 18874372
  111.9 0.9 copy-start.3
  114.0 18.5 %all-to-all-start.2 = ((bf16[2,32,16,256]{3,2,0,1:T(8,128)(2,1)}), bf16[2,32,16,256]{3,2,0,1:T(8,128)(2,1)S(1)}, u32[]{:S(2)}, u32[]{:S(2)}) async-start(bf16[2,32,16,256]{3,2,0,1:T(8,128)(2,1)} %copy.62), calls=%async_computation.2 | async-start | bytes 1048576 | tf_op jit(solution)/shard_map/all_to_all | solution.py:96
  132.8 10.9 %slice-start = ((s8[6291456]{0:T(1024)(128)(4,1)}), s8[2097152]{0:T(1024)(128)(4,1)S(1)}, s32[]{:S(2)}) async-start(s8[6291456]{0:T(1024)(128)(4,1)} %bitcast.93), calls=%async_computation.4 | async-start | bytes 4194304
  133.7 14.1 %all-to-all-start.3 = ((bf16[32,1,16,256]{3,2,1,0:T(8,128)(2,1)}), bf16[32,1,16,256]{3,2,1,0:T(8,128)(2,1)}, u32[]{:S(2)}, u32[]{:S(2)}) async-start(bf16[32,1,16,256]{3,2,1,0:T(8,128)(2,1)} %copy.65), calls=%async_computation.3 | async-start | bytes 524288 | tf_op jit(solution)/shard_map/all_to_all | solution.py:109
  137.2 6.5 %slice-start.1 = ((s8[6291456]{0:T(1024)(128)(4,1)}), s8[4194304]{0:T(1024)(128)(4,1)S(1)}, s32[]{:S(2)}) async-start(s8[6291456]{0:T(1024)(128)(4,1)} %bitcast.93), calls=%async_computation.5 | async-start | bytes 8388608
where the time goes:
time: 152 us
  blocking collectives  42 us (28%)
  matrix products  24.4 us (16%)
  other arithmetic  24 us (16%)
  waiting for transfers between devices  23.6 us (16%)
  local copies, waits for them, and re-layouts  19.1 us (13%)
  starting transfers between devices  16.3 us (11%)
  between operations  2.2 us (1%)
    all_gather x1, blocking collectives, body(): requests = lax.all_gather(selections, 'cp', axis=0, tiled=True)  42 us
    all_to_all x1, waiting for transfers between devices, body(): lax.all_to_all(partials.astype(jnp.bfloat16), 'cp', split_axis=1, concat_...  15.5 us
    sub x1, other arithmetic, attend_forward(): exponent = jnp.exp(scores - row_max)  11.7 us
    unnamed x17, local copies, waits for them, and re-layouts  9.67 us
    all_to_all x1, waiting for transfers between devices, body(): lax.all_to_all(outgoing, 'cp', split_axis=0, concat_axis=2, tiled=True)  8.1 us
    all_to_all x1, starting transfers between devices, body(): lax.all_to_all(local_pairs.reshape(local_blocks, devices, piece_rows, pai...  7.33 us
    convert_element_type x1, other arithmetic, body(): grad_scores = (weights * (grad_probs - inner_sum)).astype(jnp.bfloat16)  6.82 us
    dot_general x1, matrix products, body(): jnp.einsum('hqk,kd->qhd', probs_low, block_values, preferred_element_type...  6.53 us
  transfers between devices with their start and end apart: 4, of which 2 were waited for; matrix products, arithmetic and copies ran while one was open for 11% of the time, Pallas kernels for 0%

commit v1 on v0

--- a/solution.py
+++ b/solution.py
@@ -59,7 +59,13 @@
     held_pieces = spread.reshape(local_blocks * devices, piece_rows, pair_width)
     wanted = jnp.maximum(requests, 0)
     outgoing = held_pieces[wanted]
-    arrived = lax.all_to_all(outgoing, "cp", split_axis=0, concat_axis=2, tiled=True)
+    bring_the_body = lambda z_in, mesh_name: jnp.concatenate(
+        lax.all_to_all(
+            jnp.stack(jnp.split(z_in, lax.axis_size(mesh_name), axis=0)), mesh_name, 0, 0
+        ),
+        axis=2,
+    )
+    arrived = bring_the_body(outgoing, "cp")
     fetched = arrived.reshape(2 * local_blocks, BLK, pair_width)
     member = 0
     block_keys, block_values, allowed = block_inputs(member, fetched)

time: 152 us -> 171 us (1.12)
  local copies, waits for them, and re-layouts: 19.1 us -> 37.6 us
    unnamed x17 -> x48, local copies, waits for them, and re-layouts: 9.67 us -> 28.3 us
  transfers between devices with their start and end apart: 4 -> 4, of which waited for: 2 -> 2; matrix products, arithmetic and copies ran while one was open for 11% -> 10% of each run, Pallas kernels for 0% -> 0%
where the time goes in v1:
time: 171 us; the launch traced here: 170 us
  blocking collectives  42 us (25%)
  local copies, waits for them, and re-layouts  37.6 us (22%)
  matrix products  24.6 us (14%)
  other arithmetic  23.9 us (14%)
  waiting for transfers between devices  23.6 us (14%)
  starting transfers between devices  16.3 us (10%)
  between operations  2.22 us (1%)
    all_gather x1, blocking collectives, body(): requests = lax.all_gather(selections, 'cp', axis=0, tiled=True)  42 us
    unnamed x48, local copies, waits for them, and re-layouts  28.3 us
    all_to_all x1, waiting for transfers between devices, body(): lax.all_to_all(partials.astype(jnp.bfloat16), 'cp', split_axis=1, concat_...  15.5 us
    sub x1, other arithmetic, attend_forward(): exponent = jnp.exp(scores - row_max)  11.7 us
    all_to_all x1, waiting for transfers between devices, body(): lax.all_to_all(jnp.stack(jnp.split(z_in, lax.axis_size(mesh_name), axis=0...  8.1 us
    all_to_all x1, starting transfers between devices, body(): lax.all_to_all(local_pairs.reshape(local_blocks, devices, piece_rows, pai...  7.33 us
    convert_element_type x1, other arithmetic, body(): grad_scores = (weights * (grad_probs - inner_sum)).astype(jnp.bfloat16)  6.69 us
    dot_general x1, matrix products, body(): jnp.einsum('hqk,kd->qhd', probs_low, block_values, preferred_element_type...  6.53 us
  transfers between devices with their start and end apart: 4, of which 2 were waited for; matrix products, arithmetic and copies ran while one was open for 10% of the time, Pallas kernels for 0%

profile of v1, /device:TPU:0, one launch (start us, length us, event | category | flops | bytes accessed | tf_op | source)
XLA Modules:
  0.0 170.2 jit_solution(15794489548778190725)
XLA Ops:
  0.6 1.6 constant_dynamic-update-slice_fusion.1
  2.2 1.6 constant_dynamic-update-slice_fusion
  3.8 7.3 %all-to-all-start = ((bf16[1,32,16,256]{3,2,0,1:T(8,128)(2,1)}), bf16[1,32,16,256]{3,2,0,1:T(8,128)(2,1)S(1)}, u32[]{:S(2)}, u32[]{:S(2)}) async-start(bf16[1,32,16,256]{3,2,0,1:T(8,128)(2,1)} %bitcast.1), calls=%async_computation | async-start | bytes 524288 | tf_op jit(solution)/shard_map/all_to_all | solution.py:52
  11.1 42.0 %all-gather = s32[32,1,2]{2,1,0:T(1,128)S(1)} all-gather(s32[1,1,2]{2,1,0:T(1,128)} %bitcast.233), channel_id=1, replica_groups=mesh['cp'=32] {'cp'}, dimensions={0}, use_global_device_ids=true | all-gather | bytes 264 | tf_op jit(solution)/shard_map/all_gather | solution.py:43
  54.0 0.6 constant_dynamic-update-slice_fusion.33
  54.6 0.6 constant_dynamic-update-slice_fusion.32
  55.2 0.6 constant_dynamic-update-slice_fusion.31
  55.8 0.6 constant_dynamic-update-slice_fusion.30
  56.4 0.6 constant_dynamic-update-slice_fusion.29
  57.0 0.6 constant_dynamic-update-slice_fusion.28
  57.6 0.6 constant_dynamic-update-slice_fusion.27
  58.2 0.6 constant_dynamic-update-slice_fusion.26
  58.8 0.6 constant_dynamic-update-slice_fusion.25
  59.5 0.6 constant_dynamic-update-slice_fusion.24
  60.1 0.6 constant_dynamic-update-slice_fusion.23
  60.7 0.6 constant_dynamic-update-slice_fusion.22
  61.3 0.6 constant_dynamic-update-slice_fusion.21
  61.9 0.6 constant_dynamic-update-slice_fusion.20
  62.5 0.6 constant_dynamic-update-slice_fusion.19
  63.1 0.6 constant_dynamic-update-slice_fusion.18
  63.7 0.6 constant_dynamic-update-slice_fusion.17
  64.3 0.6 constant_dynamic-update-slice_fusion.16
  64.9 0.6 constant_dynamic-update-slice_fusion.15
  65.5 0.6 constant_dynamic-update-slice_fusion.14
  66.1 0.6 constant_dynamic-update-slice_fusion.13
  66.7 0.6 constant_dynamic-update-slice_fusion.12
  67.3 0.6 constant_dynamic-update-slice_fusion.11
  67.9 0.6 constant_dynamic-update-slice_fusion.10
  68.6 0.6 constant_dynamic-update-slice_fusion.9
  69.2 0.6 constant_dynamic-update-slice_fusion.8
  69.8 0.6 constant_dynamic-update-slice_fusion.7
  70.4 0.6 constant_dynamic-update-slice_fusion.6
  71.0 0.6 constant_dynamic-update-slice_fusion.5
  71.6 0.6 constant_dynamic-update-slice_fusion.4
  72.2 0.6 constant_dynamic-update-slice_fusion.3
  72.8 0.6 constant_dynamic-update-slice_fusion.2
  73.4 2.6 %all-to-all-start.1 = ((bf16[32,1,2,16,256]{4,3,2,1,0:T(8,128)(2,1)}), bf16[32,1,2,16,256]{4,3,2,1,0:T(8,128)(2,1)S(1)}, u32[]{:S(2)}, u32[]{:S(2)}) async-start(bf16[32,1,2,16,256]{4,3,2,1,0:T(8,128)(2,1)} %constant_dynamic-update-slice_fusion.2), calls=%async_computation.1 | async-start | bytes 1048576 | tf_op jit(solution)/shard_map/all_to_all | solution.py:63
  76.0 1.3 copy.142
  77.3 1.3 fusion.37
  79.9 1.3 copy.143
  81.3 2.2 %add_add_fusion = pred[512,1536]{0,1:T(8,128)(4,1)} fusion(pred[512,512]{0,1:T(8,128)(4,1)S(1)} %iota_compare_fusion, pred[1536]{0:T(1024)(128)(4,1)S(1)} %pad.6.clone, pred[1536]{0:T(1024)(128)(4,1)S(1)} %pad.5.clone), kind=kLoop, calls=%fused_computation.18 | loop fusion | flops 1572864 | bytes 1051648 | tf_op jit(solution)/shard_map/concatenate | solution.py:18
  83.5 8.1 %all-to-all-done.1 = bf16[32,1,2,16,256]{4,3,2,1,0:T(8,128)(2,1)S(1)} async-done(((bf16[32,1,2,16,256]{4,3,2,1,0:T(8,128)(2,1)}), bf16[32,1,2,16,256]{4,3,2,1,0:T(8,128)(2,1)S(1)}, u32[]{:S(2)}, u32[]{:S(2)}) %all-to-all-start.1) | async-done | bytes 524320 | tf_op jit(solution)/shard_map/all_to_all | solution.py:63
  91.7 1.0 pad_maximum_fusion.1
  92.7 6.3 %fusion.28 = f32[1536,512,4]{1,0,2:T(8,128)} fusion(bf16[512,4,128]{0,2,1:T(8,128)(2,1)S(1)} %bitcast.221, bf16[1536,256]{1,0:T(8,128)(2,1)S(1)} %pad_maximum_fusion.1), kind=kOutput, calls=%fused_computation.42 | convolution fusion | flops 805306368 | bytes 13500416 | tf_op jit(solution)/shard_map/qhd,kd->hqk/dot_general | solution.py:25
  99.0 11.7 %fusion.38 = (f32[4,512]{1,0:T(4,128)S(1)}, f32[4,512,1536]{1,2,0:T(8,128)S(1)}) fusion(f32[1536,512,4]{1,0,2:T(8,128)} %fusion.28, pred[512,1536]{0,1:T(8,128)(4,1)} %add_add_fusion), kind=kOutput, calls=%fused_computation.121 | output fusion | flops 18875904 | bytes 25960448 | tf_op jit(solution)/shard_map/sub | solution.py:30
  110.7 2.2 %fusion.12 = f32[1536,128]{0,1:T(8,128)S(1)} fusion(bf16[512,4,128]{0,2,1:T(8,128)(2,1)S(1)} %bitcast.230, f32[4,512,1536]{1,2,0:T(8,128)S(1)} %get-tuple-element.25, f32[4,512]{1,0:T(4,128)S(1)} %get-tuple-element.24), kind=kOutput, calls=%fused_computation.19 | convolution fusion | flops 811597824 | bytes 13901824 | tf_op jit(solution)/shard_map/hqk,qhd->kd/dot_general | solution.py:96
  112.9 6.1 %fusion.1 = (f32[4,512]{1,0:T(4,128)S(1)}, f32[1536,512,4]{1,0,2:T(8,128)}) fusion(f32[4,512,1536]{1,2,0:T(8,128)S(1)} %get-tuple-element.25, f32[4,512]{1,0:T(4,128)S(1)} %get-tuple-element.24, bf16[512,4,128]{0,2,1:T(8,128)(2,1)S(1)} %bitcast.231, bf16[1536,256]{1,0:T(8,128)(2,1)S(1)} %pad_maximum_fusion.1), kind=kOutput, calls=%fused_computation.4 | convolution fusion | flops 814741504 | bytes 26099712 | tf_op jit(solution)/shard_map/qhd,kd->hqk/dot_general | solution.py:82
  119.0 6.7 %fusion.3 = bf16[4,512,1536]{1,2,0:T(8,128)(2,1)S(1)} fusion(f32[1536,512,4]{1,0,2:T(8,128)} %get-tuple-element.27, f32[4,512]{1,0:T(4,128)S(1)} %get-tuple-element.26, f32[4,512,1536]{1,2,0:T(8,128)S(1)} %get-tuple-element.25, f32[4,512]{1,0:T(4,128)S(1)} %get-tuple-element.24), kind=kLoop, calls=%fused_computation.6 | loop fusion | flops 12582912 | bytes 31473664 | tf_op jit(solution)/shard_map/convert_element_type | solution.py:86
  125.7 2.6 %copy-done = bf16[4,512,1536]{1,2,0:T(8,128)(2,1)} copy-done((bf16[4,512,1536]{1,2,0:T(8,128)(2,1)}, bf16[4,512,1536]{1,2,0:T(8,128)(2,1)S(1)}, u32[]{:S(2)}) %copy-start) | copy-done | bytes 6291480
  128.3 2.1 %fusion.15 = f32[1536,128]{0,1:T(8,128)S(1)} fusion(bf16[4,512,1536]{1,2,0:T(8,128)(2,1)S(1)} %fusion.3, bf16[512,4,128]{0,2,1:T(8,128)(2,1)S(1)} %bitcast.222), kind=kOutput, calls=%fused_computation.21 | convolution fusion | flops 805502976 | bytes 7602176 | tf_op jit(solution)/shard_map/hqk,qhd->kd/dot_general | solution.py:93
  130.5 0.8 copy-done.3
  131.7 0.9 copy.124
  132.5 2.9 %all-to-all-start.2 = ((bf16[2,32,16,256]{3,2,0,1:T(8,128)(2,1)}), bf16[2,32,16,256]{3,2,0,1:T(8,128)(2,1)S(1)}, u32[]{:S(2)}, u32[]{:S(2)}) async-start(bf16[2,32,16,256]{3,2,0,1:T(8,128)(2,1)} %copy.124), calls=%async_computation.2 | async-start | bytes 1048576 | tf_op jit(solution)/shard_map/all_to_all | solution.py:102
  135.5 15.5 %all-to-all-done.2 = bf16[2,32,16,256]{3,2,0,1:T(8,128)(2,1)S(1)} async-done(((bf16[2,32,16,256]{3,2,0,1:T(8,128)(2,1)}), bf16[2,32,16,256]{3,2,0,1:T(8,128)(2,1)S(1)}, u32[]{:S(2)}, u32[]{:S(2)}) %all-to-all-start.2) | async-done | bytes 524320 | tf_op jit(solution)/shard_map/all_to_all | solution.py:102
  151.4 0.9 copy.127
  152.2 3.5 %all-to-all-start.3 = ((bf16[32,1,16,256]{3,2,1,0:T(8,128)(2,1)}), bf16[32,1,16,256]{3,2,1,0:T(8,128)(2,1)}, u32[]{:S(2)}, u32[]{:S(2)}) async-start(bf16[32,1,16,256]{3,2,1,0:T(8,128)(2,1)} %copy.127), calls=%async_computation.3 | async-start | bytes 524288 | tf_op jit(solution)/shard_map/all_to_all | solution.py:115
  155.7 6.5 %fusion.18 = bf16[128,4,512]{2,0,1:T(8,128)(2,1)} fusion(bf16[1536,256]{1,0:T(8,128)(2,1)S(1)} %pad_maximum_fusion.1, f32[4,512,1536]{1,2,0:T(8,128)} %copy-done.1, f32[4,512]{1,0:T(4,128)S(1)} %get-tuple-element.24), kind=kOutput, calls=%fused_computation.28 | convolution fusion | flops 811859968 | bytes 13508608 | tf_op jit(solution)/shard_map/hqk,kd->qhd/dot_general | solution.py:73
  162.3 1.0 fusion.17
  163.3 1.0 copy.131
  164.3 2.0 %copy.130 = bf16[512,512]{1,0:T(8,128)(2,1)} copy(bf16[512,512]{0,1:T(8,128)(2,1)} %bitcast.232) | data formatting | bytes 1048576
  166.3 1.0 bitcast_convert_fusion
  167.5 1.1 fusion.24
  168.7 0.8 copy.132
  169.4 0.8 copy.133
  (35 shorter events, 2.1 us)
Async XLA Ops:
  3.8 49.6 %all-to-all-start = ((bf16[1,32,16,256]{3,2,0,1:T(8,128)(2,1)}), bf16[1,32,16,256]{3,2,0,1:T(8,128)(2,1)S(1)}, u32[]{:S(2)}, u32[]{:S(2)}) async-start(bf16[1,32,16,256]{3,2,0,1:T(8,128)(2,1)} %bitcast.1), calls=%async_computation | async-start | bytes 524288 | tf_op jit(solution)/shard_map/all_to_all | solution.py:52
  73.4 18.2 %all-to-all-start.1 = ((bf16[32,1,2,16,256]{4,3,2,1,0:T(8,128)(2,1)}), bf16[32,1,2,16,256]{4,3,2,1,0:T(8,128)(2,1)S(1)}, u32[]{:S(2)}, u32[]{:S(2)}) async-start(bf16[32,1,2,16,256]{4,3,2,1,0:T(8,128)(2,1)} %constant_dynamic-update-slice_fusion.2), calls=%async_computation.1 | async-start | bytes 1048576 | tf_op jit(solution)/shard_map/all_to_all | solution.py:63
  110.6 8.3 %copy-start.1 = (f32[4,512,1536]{1,2,0:T(8,128)}, f32[4,512,1536]{1,2,0:T(8,128)S(1)}, u32[]{:S(2)}) copy-start(f32[4,512,1536]{1,2,0:T(8,128)S(1)} %get-tuple-element.25) | copy-start | bytes 37748740
  112.9 17.5 %copy-start.2 = (f32[1536,128]{0,1:T(8,128)}, f32[1536,128]{0,1:T(8,128)S(1)}, u32[]{:S(2)}) copy-start(f32[1536,128]{0,1:T(8,128)S(1)} %fusion.12) | copy-start | bytes 2359300
  125.7 2.6 %copy-start = (bf16[4,512,1536]{1,2,0:T(8,128)(2,1)}, bf16[4,512,1536]{1,2,0:T(8,128)(2,1)S(1)}, u32[]{:S(2)}) copy-start(bf16[4,512,1536]{1,2,0:T(8,128)(2,1)S(1)} %fusion.3) | copy-start | bytes 18874372
  130.4 0.9 copy-start.3
  132.5 18.5 %all-to-all-start.2 = ((bf16[2,32,16,256]{3,2,0,1:T(8,128)(2,1)}), bf16[2,32,16,256]{3,2,0,1:T(8,128)(2,1)S(1)}, u32[]{:S(2)}, u32[]{:S(2)}) async-start(bf16[2,32,16,256]{3,2,0,1:T(8,128)(2,1)} %copy.124), calls=%async_computation.2 | async-start | bytes 1048576 | tf_op jit(solution)/shard_map/all_to_all | solution.py:102
  151.3 10.9 %slice-start = ((s8[6291456]{0:T(1024)(128)(4,1)}), s8[2097152]{0:T(1024)(128)(4,1)S(1)}, s32[]{:S(2)}) async-start(s8[6291456]{0:T(1024)(128)(4,1)} %bitcast.218), calls=%async_computation.4 | async-start | bytes 4194304
  152.2 14.1 %all-to-all-start.3 = ((bf16[32,1,16,256]{3,2,1,0:T(8,128)(2,1)}), bf16[32,1,16,256]{3,2,1,0:T(8,128)(2,1)}, u32[]{:S(2)}, u32[]{:S(2)}) async-start(bf16[32,1,16,256]{3,2,1,0:T(8,128)(2,1)} %copy.127), calls=%async_computation.3 | async-start | bytes 524288 | tf_op jit(solution)/shard_map/all_to_all | solution.py:115
  155.7 6.5 %slice-start.1 = ((s8[6291456]{0:T(1024)(128)(4,1)}), s8[4194304]{0:T(1024)(128)(4,1)S(1)}, s32[]{:S(2)}) async-start(s8[6291456]{0:T(1024)(128)(4,1)} %bitcast.218), calls=%async_computation.5 | async-start | bytes 8388608
